TPU v7x, 32 devices: a whole 2x2x4 slice. The times are simulated.
32 devices in a mesh: pts: 8 (over z, y), grp: 4 (over x, core).
Axes of the slice: x: 2, y: 2, z: 4, core: 2. Of those that a mesh axis runs over, the one named last changes fastest.
Arguments:
- jacobian: bfloat16 [4096, 3, 3, 384], P(('pts', 'grp')), may hold values from -0.15625 to 0.15625
- owner: int32 [4096, 1], P(('pts', 'grp')), may hold values from 0 to 7; in each aligned block of 128 rows (0 to 127, 128 to 255, ...) at most 32 rows name the same one
- damping: float32 [8, 384], P('pts'), may hold values from 0.2 to 2
Outputs:
- reduced_diag: float32 [8, 384, 384], P('pts', None, 'grp')
- reduced_pair: float32 [8, 384, 384], P('pts', None, 'grp')
Inputs may be any that keep to these rules, and one draw needn't show every extreme that they name: `owner`: among the 128 landmarks of one device at most 32 name the same segment, and in every draw some segment is named by exactly 32 landmarks of some device.
All inputs are finite; a program needn't handle non-finite values.
Results may differ from a plain program's by a relative error of at most 0.0003.
Values may be sent and summed in bfloat16 or wider, within the bound.
A program may use at most 64 MiB of HBM per device.

v0:
```python
import jax
import jax.numpy as jnp
from jax import lax
from jax.sharding import PartitionSpec as P


def shifted(value, axis, by):
    devices = lax.axis_size(axis)
    return lax.ppermute(value, axis, [(i, (i + by) % devices) for i in range(devices)])


def gram(left, right):
    return lax.dot_general(
        left, right, (((0,), (0,)), ((), ())), preferred_element_type=jnp.float32
    )


def exact_gram(left, right):
    return lax.dot_general(
        left,
        right,
        (((0,), (0,)), ((), ())),
        precision=lax.Precision.HIGHEST,
        preferred_element_type=jnp.float32,
    )


def local(jacobian, owner, damping):
    points = jacobian.shape[0]
    width = jacobian.shape[3]
    owners = lax.axis_size("pts")
    groups = lax.axis_size("grp")
    capacity = max(2, 2 * points // owners)
    slots = owners * capacity
    segment = owner[:, 0]
    same = segment[:, None] == segment[None, :]
    before = jnp.arange(points)[None, :] < jnp.arange(points)[:, None]
    rank = jnp.sum((same & before).astype(jnp.int32), axis=1)
    slot_of = segment * capacity + rank
    match = slot_of[None, :] == jnp.arange(slots, dtype=jnp.int32)[:, None]
    source = jnp.sum(match.astype(jnp.int32) * jnp.arange(points, dtype=jnp.int32)[None, :], axis=1)
    filled = jnp.any(match, axis=1)
    outgoing = jnp.where(
        filled[:, None, None, None], jacobian[source], jnp.zeros((), jacobian.dtype)
    )
    received = lax.all_to_all(outgoing, "pts", split_axis=0, concat_axis=0, tiled=True)
    columns = width // groups
    col_start = lax.axis_index("grp") * columns
    first = received[:, 0].reshape(-1, width)
    middle = received[:, 1].reshape(-1, width)
    last = received[:, 2].reshape(-1, width)
    d_odd, b_low, b_high = lax.psum(
        (gram(middle, middle), gram(middle, first), gram(middle, last)), "grp"
    )
    d_low, d_high, e_pair = (
        lax.psum_scatter(gram(first, first), "grp", scatter_dimension=1, tiled=True),
        lax.psum_scatter(gram(last, last), "grp", scatter_dimension=1, tiled=True),
        lax.psum_scatter(gram(first, last), "grp", scatter_dimension=1, tiled=True),
    )
    system = d_odd + jnp.diag(damping[0])
    factor = jnp.linalg.cholesky(system)
    y_low = lax.linalg.triangular_solve(factor, b_low, left_side=True, lower=True)
    y_high = lax.linalg.triangular_solve(factor, b_high, left_side=True, lower=True)
    y_low_cols = lax.dynamic_slice_in_dim(y_low, col_start, columns, 1)
    y_high_cols = lax.dynamic_slice_in_dim(y_high, col_start, columns, 1)
    low = d_low - exact_gram(y_low, y_low_cols)
    high = d_high - exact_gram(y_high, y_high_cols)
    pair = e_pair - exact_gram(y_low, y_high_cols)
    carried = shifted(high, "pts", 1)
    return ((low + carried)[None], pair[None])


def solution(mesh):
    placed = (P(("pts", "grp"), None, None, None), P(("pts", "grp"), None), P("pts", None))
    return jax.shard_map(
        local,
        mesh=mesh,
        in_specs=placed,
        out_specs=(P("pts", None, "grp"), P("pts", None, "grp")),
        check_vma=False,
    )
```

profile of v0, /device:TPU:0, one launch (start us, length us, event | category | flops | bytes accessed | tf_op | source)
XLA Modules:
  0.0 261.4 jit_solution(13856326678899369149)
XLA Ops:
  7.2 0.9 convert_reduce_fusion
  8.1 0.7 multiply_add_fusion
  9.1 6.1 %gather_fusion = bf16[256,3,3,384]{3,0,2,1:T(8,128)(2,1)S(1)} fusion(bf16[128,3,3,384]{3,0,2,1:T(8,128)(2,1)S(1)} %copy-done, s32[1024]{0:T(1024)S(1)} %pad_clamp_fusion), kind=kCustom, calls=%fused_computation | custom fusion | bytes 3539968 | tf_op jit(solution)/shard_map/gather | solution.py:44
  15.5 1.5 copy.57
  17.0 61.0 %all_to_all.5 = bf16[256,3,3,384]{3,2,1,0:T(4,128)(2,1)S(1)} all-to-all(bf16[256,3,3,384]{3,2,1,0:T(4,128)(2,1)S(1)} %copy.57), channel_id=1, replica_groups=mesh['pts'=8,'grp'=4] {'pts'}, dimensions={0} | all-to-all | bytes 3538944 | tf_op jit(solution)/shard_map/all_to_all | solution.py:46
  78.0 2.0 fusion.46
  79.9 1.5 copy.90
  81.4 1.3 convolution_bitcast_fusion.4
  82.8 1.3 convolution_bitcast_fusion.3
  84.1 1.5 copy.92
  85.6 1.4 convolution_bitcast_fusion.1
  87.0 1.3 convolution_bitcast_fusion.2
  88.5 1.3 convolution_bitcast_fusion
  89.8 0.3 reduce-scatter.4.cloned.1.call-start
  90.2 1.3 convolution_bitcast_fusion.5
  91.5 40.8 %all-reduce.4.cloned.1.call-done = (f32[384,384]{1,0:T(8,128)}, f32[384,384]{0,1:T(8,128)}, f32[384,384]{1,0:T(8,128)}) async-done(((f32[384,384]{1,0:T(8,128)}, f32[384,384]{0,1:T(8,128)}, f32[384,384]{1,0:T(8,128)}), (f32[384,384]{1,0:T(8,128)}, f32[384,384]{0,1:T(8,128)}, f32[384,384]{1,0:T(8,128)})) %all-reduce.4.cloned.1.call-update) | async-done | bytes 1769488 | tf_op jit(solution)/shard_map/psum | solution.py:52
  132.3 1.2 select_add_fusion
  133.8 11.7 %cholesky.76 = f32[128,128]{1,0:T(8,128)S(1)} custom-call(f32[128,128]{1,0:T(8,128)S(1)} %cholesky.189), custom_call_target="Cholesky" | custom-call | tf_op jit(solution)/shard_map/jit(cholesky)/cholesky | solution.py:61
  145.5 9.8 %custom-call.22 = f32[1,128,128]{1,2,0:T(8,128)S(1)} custom-call(f32[1,128,128]{2,1,0:T(8,128)S(1)} %get-tuple-element.70), custom_call_target="InvertDiagBlocksLowerTriangular" | custom-call | tf_op jit(solution)/shard_map/jit(cholesky)/cholesky | solution.py:61
  155.9 11.7 %cholesky.160 = f32[128,128]{1,0:T(8,128)S(1)} custom-call(f32[128,128]{1,0:T(8,128)S(1)} %cholesky.193), custom_call_target="Cholesky" | custom-call | tf_op jit(solution)/shard_map/jit(cholesky)/cholesky | solution.py:61
  168.0 19.3 %custom-call.23 = f32[1,128,128]{1,2,0:T(8,128)S(1)} custom-call(f32[1,128,128]{2,1,0:T(8,128)S(1)} %get-tuple-element.68), custom_call_target="InvertDiagBlocksLowerTriangular" | custom-call | tf_op jit(solution)/shard_map/jit(cholesky)/cholesky | solution.py:61
  187.7 0.4 convolution_subtract_fusion.8
  188.0 11.7 %cholesky.179 = f32[128,128]{1,0:T(8,128)S(1)} custom-call(f32[128,128]{1,0:T(8,128)S(1)} %convolution_subtract_fusion.8), custom_call_target="Cholesky" | custom-call | tf_op jit(solution)/shard_map/jit(cholesky)/cholesky | solution.py:61
  199.9 0.6 compare_reduce_fusion
  200.5 0.7 compare_reduce_fusion.1
  203.1 6.1 %while.4 = (s32[]{:T(128)}, f32[384,384]{0,1:T(8,128)S(1)}, s32[3,2]{0,1:T(2,128)S(1)}, f32[3,128,128]{2,1,0:T(8,128)S(1)}, s32[]{:T(128)}) while((s32[]{:T(128)}, f32[384,384]{0,1:T(8,128)S(1)}, s32[3,2]{0,1:T(2,128)S(1)}, f32[3,128,128]{2,1,0:T(8,128)S(1)}, s32[]{:T(128)}) %tuple.41), condition=%wide.while_cond, body=%wide.while_body.sunk | while | flops 2 | bytes 393321 | solution.py:62
  203.2 0.5 fusion.57
  203.7 1.3 dynamic-slice.9
  205.2 0.5 fusion.57
  205.8 1.3 dynamic-slice.9
  207.3 0.5 fusion.57
  207.8 1.3 dynamic-slice.9
  209.2 29.5 %custom-call.25 = f32[3,128,128]{1,2,0:T(8,128)S(1)} custom-call(f32[3,128,128]{2,1,0:T(8,128)S(1)} %get-tuple-element.17), custom_call_target="InvertDiagBlocksLowerTriangular" | custom-call | tf_op jit(solution)/shard_map/triangular_solve/custom-call.2 | solution.py:62
  238.8 0.4 fusion.18
  239.1 0.4 convolution_subtract_fusion.3
  239.5 0.4 fusion.16
  239.9 0.4 convolution_subtract_fusion.1
  240.3 0.4 fusion.34
  240.6 0.4 convolution_subtract_fusion
  241.1 0.4 fusion.36
  241.5 0.4 fusion.35
  241.9 0.4 convolution_subtract_fusion.2
  242.3 0.4 fusion.37
  242.7 1.6 convolution_subtract_fusion.5
  244.3 1.5 collective-permute-start
  245.9 2.2 fusion
  248.1 4.3 %collective-permute-done = f32[384,96]{0,1:T(8,128)S(1)} collective-permute-done((f32[384,96]{0,1:T(8,128)S(1)}, f32[384,96]{0,1:T(8,128)S(1)}, u32[]{:S(2)}, u32[]{:S(2)}) %collective-permute-start) | collective-permute-done | bytes 147488 | tf_op jit(solution)/shard_map/ppermute | solution.py:9
  252.5 2.2 fusion.2
  (59 shorter events, 3.1 us)
Async XLA Ops:
  7.2 1.9 copy-start
  7.2 125.1 %all-reduce.4.cloned.1.call-start = ((), (), s32[]{:S(2)}) async-start(), calls=%async_computation.7 | async-start | bytes 3538944 | tf_op jit(solution)/shard_map/psum | solution.py:52
  87.0 155.7 %reduce-scatter.6.cloned.1.call-start = ((), (), s32[]{:S(2)}) async-start(), calls=%async_computation.5 | async-start | bytes 737280 | tf_op jit(solution)/shard_map/reduce_scatter | solution.py:57
  88.4 1.7 copy-start.4
  88.4 157.5 %reduce-scatter.8.cloned.1.call-start = ((), (), s32[]{:S(2)}) async-start(), calls=%async_computation.6 | async-start | bytes 737280 | tf_op jit(solution)/shard_map/reduce_scatter | solution.py:58
  89.8 158.3 %reduce-scatter.4.cloned.1.call-start = ((), (), s32[]{:S(2)}) async-start(), calls=%async_computation.4 | async-start | bytes 737280 | tf_op jit(solution)/shard_map/reduce_scatter | solution.py:56
  132.3 1.4 copy-start.1
  199.9 38.9 %copy-start.2 = (f32[384,384]{1,0:T(8,128)S(1)}, f32[384,384]{1,0:T(8,128)}, u32[]{:S(2)}) copy-start(f32[384,384]{1,0:T(8,128)} %get-tuple-element.61) | copy-start | bytes 1769476
  203.1 36.4 %copy-start.3 = (f32[384,384]{1,0:T(8,128)S(1)}, f32[384,384]{1,0:T(8,128)}, u32[]{:S(2)}) copy-start(f32[384,384]{1,0:T(8,128)} %get-tuple-element.59) | copy-start | bytes 1769476
  244.3 8.2 %collective-permute-start = (f32[384,96]{0,1:T(8,128)S(1)}, f32[384,96]{0,1:T(8,128)S(1)}, u32[]{:S(2)}, u32[]{:S(2)}) collective-permute-start(f32[384,96]{0,1:T(8,128)S(1)} %convolution_subtract_fusion.5), channel_id=1, source_target_pairs={{0,4},{4,8},{8,12},{12,16},{16,20},{20,24},{24,28},{28,0},{1,5},{5... | collective-permute-start | bytes 442376 | tf_op jit(solution)/shard_map/ppermute | solution.py:9
Sparse Core Ops, SparseCore 0:
  87.1 45.0 all-reduce.3
  134.8 22.2 reduce-scatter.5
  159.6 22.2 reduce-scatter.7
  184.2 22.1 reduce-scatter.3
where the time goes:
time: 265 us; the launch traced here: 261 us
  other arithmetic  98.6 us (37%)
  blocking collectives  61 us (23%)
  waiting for transfers between devices  45.2 us (17%)
  local copies, waits for them, and re-layouts  19.3 us (7%)
  matrix products  19.1 us (7%)
  between operations  16.2 us (6%)
    another operation x10, other arithmetic, local(): factor = jnp.linalg.cholesky(system)  65.6 us
    all_to_all x1, blocking collectives, local(): lax.all_to_all(outgoing, 'pts', split_axis=0, concat_axis=0, tiled=True)  61 us
    psum x1, waiting for transfers between devices, local(): lax.psum((gram(middle, middle), gram(middle, first), gram(middle, last)),...  40.8 us
    another operation x5, other arithmetic, local(): lax.linalg.triangular_solve(factor, b_low, left_side=True, lower=True)  29.6 us
    dot_general x6, matrix products, gram(): lax.dot_general(left, right, (((0,), (0,)), ((), ())), preferred_element_...  8 us
    gather x1, local copies, waits for them, and re-layouts, local(): jacobian[source]  6.13 us
    dot_general x3, matrix products, exact_gram(): lax.dot_general(left, right, (((0,), (0,)), ((), ())), precision=lax.Prec...  6.02 us
    another operation x16, local copies, waits for them, and re-layouts, local(): lax.linalg.triangular_solve(factor, b_low, left_side=True, lower=True)  6 us
  transfers between devices with their start and end apart: 5, of which 2 were waited for; matrix products, arithmetic and copies ran while one was open for 44% of the time, Pallas kernels for 0%

commit v1 on v0

v1 whole, which is shorter than its diff:
```python
import functools

import jax
import jax.numpy as jnp
from jax import lax
from jax.experimental import pallas as pl
from jax.experimental.pallas import tpu as pltpu
from jax.sharding import PartitionSpec as P

MESH = pl.DeviceIdType.MESH
LANES = 128
TILE = 8


def mm(left, right, dims, precise):
    return lax.dot_general(
        left,
        right,
        (dims, ((), ())),
        precision=lax.Precision.HIGHEST if precise else None,
        preferred_element_type=jnp.float32,
    )


NN = ((1,), (0,))
NT = ((1,), (1,))
TN = ((0,), (0,))


def sweep_steps(matrix, rounds):
    size = matrix.shape[0]
    lane_row = lax.broadcasted_iota(jnp.int32, (1, size), 1)
    lane = lax.broadcasted_iota(jnp.int32, (size, size), 1)
    top_row = lax.broadcasted_iota(jnp.int32, (TILE, size), 0)

    def body(_, a):
        for t in range(TILE):
            row = a[t : t + 1, :]
            col = a[:, t : t + 1]
            scaled = jnp.where(lane_row == t, -1.0, row) * (1.0 / a[t : t + 1, t : t + 1])
            new = jnp.where(lane == t, 0.0, a) - col * scaled
            top = jnp.where(top_row == t, scaled, new[:TILE])
            a = jnp.concatenate([top, new[TILE:]], 0)
        a = pltpu.roll(a, size - TILE, 1)
        return jnp.concatenate([a[TILE:], a[:TILE]], 0)

    return lax.fori_loop(0, rounds, body, matrix)


def kernel(
    owners, groups, rows_per, width,
    send, damp, diag_out, pair_out,
    recv, sblk, s1, s2, gram, r1, r2, bt, highs, carried,
    a_send, a_recv, d_send, d_recv, d2_recv, g_send, g_recv, b_send, b_recv, c_send, c_recv, own_sem,
):
    me = lax.axis_index("pts")
    grp = lax.axis_index("grp")
    near = grp + 1 - 2 * lax.rem(grp, 2)
    far = lax.rem(grp + 2, groups)
    chunk = width // groups
    nb = width // LANES
    pairs = [(i, j) for i in range(nb) for j in range(i, nb)]
    odd = lax.rem(grp, 2)

    barrier = pltpu.get_barrier_semaphore()

    def greet(off, _):
        pl.semaphore_signal(
            barrier, inc=1, device_id=(lax.rem(me + off, owners), grp), device_id_type=MESH
        )
        return 0

    lax.fori_loop(1, owners, greet, 0)
    for other in (near, far):
        pl.semaphore_signal(barrier, inc=1, device_id=(me, other), device_id_type=MESH)
    pl.semaphore_wait(barrier, owners - 1 + 2)

    def rows_at(i):
        return pl.ds(pl.multiple_of(i * rows_per, rows_per), rows_per)

    for k in (1, 0, 2):
        def issue(off, _, k=k):
            to = lax.rem(me + off, owners)
            pltpu.make_async_remote_copy(
                src_ref=send.at[k, rows_at(to)],
                dst_ref=recv.at[k, rows_at(me)],
                send_sem=a_send.at[k],
                recv_sem=a_recv.at[k],
                device_id=(to, grp),
                device_id_type=MESH,
            ).start()
            return 0

        lax.fori_loop(1, owners, issue, 0)
    for k in range(3):
        pltpu.make_async_copy(
            send.at[k, rows_at(me)], recv.at[k, rows_at(me)], own_sem.at[k]
        ).start()
    for k in range(3):
        pltpu.make_async_copy(
            send.at[k, rows_at(me)], recv.at[k, rows_at(me)], own_sem.at[k]
        ).wait()

    def await_rows(k):
        part = recv.at[k, pl.ds(0, (owners - 1) * rows_per)]
        pltpu.make_async_copy(part, part, a_recv.at[k]).wait()

    await_rows(1)
    first_copies = []
    for n, (i, j) in enumerate(pairs):
        sblk[n] = mm(
            recv[1, :, i * LANES : (i + 1) * LANES],
            recv[1, :, j * LANES : (j + 1) * LANES], TN, False,
        )
        copy = pltpu.make_async_remote_copy(
            src_ref=sblk.at[n], dst_ref=s1.at[n],
            send_sem=d_send.at[n], recv_sem=d_recv.at[n],
            device_id=(me, near), device_id_type=MESH,
        )
        copy.start()
        first_copies.append(copy)
    second_copies = []
    own = len(pairs)
    for n in range(own):
        first_copies[n].wait_recv()
        sblk[own + n] = sblk[n] + s1[n]
        copy = pltpu.make_async_remote_copy(
            src_ref=sblk.at[own + n], dst_ref=s2.at[n],
            send_sem=d_send.at[own + n], recv_sem=d2_recv.at[n],
            device_id=(me, far), device_id_type=MESH,
        )
        copy.start()
        second_copies.append(copy)

    eye = (
        lax.broadcasted_iota(jnp.int32, (LANES, LANES), 0)
        == lax.broadcasted_iota(jnp.int32, (LANES, LANES), 1)
    )

    def reduced(n):
        second_copies[n].wait_recv()
        i, j = pairs[n]
        total = sblk[own + n] + s2[n]
        if i == j:
            total = total + jnp.where(eye, damp[:, i * LANES : (i + 1) * LANES], 0.0)
        return total

    where_in = {pair: n for n, pair in enumerate(pairs)}
    blocks = {}
    inverses, factors = [], {}
    rounds = LANES // TILE
    half = rounds // 2

    sides = ((0, 1), (2, 1), (0, 0), (2, 2), (2, 0))
    count = len(sides)

    def chunk_rows(c):
        return pl.ds(pl.multiple_of(c * chunk, TILE), chunk)

    def make_grams():
        await_rows(0)
        await_rows(2)
        for m, (left, right) in enumerate(sides):
            gram[m] = mm(recv[left], recv[right], TN, False)
            for h in range(2):
                near_copy(m, h).start()

    def near_copy(m, h):
        return pltpu.make_async_remote_copy(
            src_ref=gram.at[m, chunk_rows(1 - odd + 2 * h)], dst_ref=r1.at[m, h],
            send_sem=g_send.at[m, h], recv_sem=g_recv.at[m, h],
            device_id=(me, near), device_id_type=MESH,
        )

    def far_copy(m):
        return pltpu.make_async_remote_copy(
            src_ref=gram.at[m, chunk_rows(far)], dst_ref=r2.at[m],
            send_sem=g_send.at[m, 2], recv_sem=g_recv.at[m, 2],
            device_id=(me, far), device_id_type=MESH,
        )

    def fold_near():
        for m in range(count):
            for h in range(2):
                near_copy(m, h).wait()
                at = chunk_rows(odd + 2 * h)
                gram[m, at, :] = gram[m, at, :] + r1[m, h]
            far_copy(m).start()

    def spread_far(m):
        return pltpu.make_async_remote_copy(
            src_ref=bt.at[m, chunk_rows(grp)], dst_ref=bt.at[m, chunk_rows(grp)],
            send_sem=b_send.at[m, 0], recv_sem=b_recv.at[m, 0],
            device_id=(me, far), device_id_type=MESH,
        )

    def spread_near(m, h):
        at = chunk_rows(odd + 2 * h)
        return pltpu.make_async_remote_copy(
            src_ref=bt.at[m, at], dst_ref=bt.at[m, at],
            send_sem=b_send.at[m, 1 + h], recv_sem=b_recv.at[m, 1 + h],
            device_id=(me, near), device_id_type=MESH,
        )

    def fold_far():
        for m in range(count):
            far_copy(m).wait()
            at = chunk_rows(grp)
            if m < 2:
                bt[m, at, :] = gram[m, at, :] + r2[m]
                spread_far(m).start()
            else:
                gram[m, at, :] = gram[m, at, :] + r2[m]

    def spread():
        for m in range(2):
            spread_far(m).wait()
            for h in range(2):
                spread_near(m, h).start()

    hooks = {(0, 1): make_grams, (1, 0): fold_near, (1, 1): fold_far, (2, 0): spread}
    for i in range(nb):
        for j in range(i, nb):
            blocks[i, j] = blocks[i, j] if i > 0 else reduced(where_in[i, j])
        if i == 0:
            for pair in pairs:
                if pair[0] > 0:
                    blocks[pair] = None
        a = sweep_steps(blocks[i, i], half)
        if (i, 0) in hooks:
            hooks.pop((i, 0))()
        a = -sweep_steps(a, rounds - half)
        if (i, 1) in hooks:
            hooks.pop((i, 1))()
        inverses.append(a)
        for j in range(i + 1, nb):
            factors[i, j] = mm(a, blocks[i, j], NN, True)
        for j in range(i + 1, nb):
            for k in range(j, nb):
                base = blocks[j, k]
                if base is None:
                    base = reduced(where_in[j, k])
                blocks[j, k] = base - mm(blocks[i, j], factors[i, k], TN, True)
    for key in sorted(hooks):
        hooks[key]()
    for m in range(2):
        for h in range(2):
            spread_near(m, h).wait()

    for m in range(2):
        for j in range(1, nb):
            value = bt[m, :, j * LANES : (j + 1) * LANES]
            for i in range(j):
                value = value - mm(
                    bt[m, :, i * LANES : (i + 1) * LANES], factors[i, j], NN, True
                )
            bt[m, :, j * LANES : (j + 1) * LANES] = value
    mine = chunk_rows(grp)
    solved = []
    for m in range(2):
        solved.append(
            jnp.concatenate(
                [
                    mm(bt[m, mine, i * LANES : (i + 1) * LANES], inverses[i], NN, True)
                    for i in range(nb)
                ],
                1,
            )
        )
    highs[...] = gram[3, mine, :] - mm(solved[1], bt[1], NT, True)
    carry = pltpu.make_async_remote_copy(
        src_ref=highs, dst_ref=carried, send_sem=c_send, recv_sem=c_recv,
        device_id=(lax.rem(me + 1, owners), grp), device_id_type=MESH,
    )
    carry.start()
    low = gram[2, mine, :] - mm(solved[0], bt[0], NT, True)
    pair_out[...] = (gram[4, mine, :] - mm(solved[1], bt[0], NT, True)).T
    for copy in first_copies + second_copies:
        copy.wait_send()
    for k in range(3):
        part = send.at[k, pl.ds(0, (owners - 1) * rows_per)]
        pltpu.make_async_copy(part, part, a_send.at[k]).wait()
    carry.wait()
    diag_out[...] = (low + carried[...]).T


def local(jacobian, owner, damping):
    points, clusters, residuals, width = jacobian.shape
    owners = lax.axis_size("pts")
    groups = lax.axis_size("grp")
    capacity = max(2, 2 * points // owners)
    rows_per = -(-residuals * capacity // 16) * 16
    total = owners * rows_per
    segment = owner[:, 0]
    same = segment[:, None] == segment[None, :]
    before = jnp.arange(points)[:, None] < jnp.arange(points)[None, :]
    rank = jnp.sum((same & before).astype(jnp.int32), axis=0)
    place = segment * rows_per + rank
    place = (place[None, :] + capacity * jnp.arange(residuals)[:, None]).reshape(-1)
    pick = (jnp.arange(total)[:, None] == place[None, :]).astype(jacobian.dtype)
    planes = jnp.transpose(jacobian, (1, 2, 0, 3)).reshape(clusters, residuals * points, width)
    outgoing = jnp.einsum(
        "qp,kpf->kqf", pick, planes, preferred_element_type=jnp.float32
    ).astype(jacobian.dtype)
    chunk = width // groups
    nb = width // LANES
    blocks = nb * (nb + 1) // 2
    vmem = pl.BlockSpec(memory_space=pltpu.VMEM)
    dma = pltpu.SemaphoreType.DMA
    diag, pair = pl.pallas_call(
        functools.partial(kernel, owners, groups, rows_per, width),
        out_shape=[jax.ShapeDtypeStruct((width, chunk), jnp.float32)] * 2,
        in_specs=[vmem, vmem],
        out_specs=[vmem, vmem],
        scratch_shapes=[
            pltpu.VMEM((clusters, total, width), jacobian.dtype),
            pltpu.VMEM((2 * blocks, LANES, LANES), jnp.float32),
            pltpu.VMEM((blocks, LANES, LANES), jnp.float32),
            pltpu.VMEM((blocks, LANES, LANES), jnp.float32),
            pltpu.VMEM((5, width, width), jnp.float32),
            pltpu.VMEM((5, 2, chunk, width), jnp.float32),
            pltpu.VMEM((5, chunk, width), jnp.float32),
            pltpu.VMEM((2, width, width), jnp.float32),
            pltpu.VMEM((chunk, width), jnp.float32),
            pltpu.VMEM((chunk, width), jnp.float32),
            dma((3,)), dma((3,)),
            dma((2 * blocks,)), dma((blocks,)), dma((blocks,)),
            dma((5, 3)), dma((5, 3)),
            dma((2, 3)), dma((2, 3)),
            dma, dma, dma((3,)),
        ],
        compiler_params=pltpu.CompilerParams(collective_id=0, has_side_effects=True),
    )(outgoing, damping)
    return diag[None], pair[None]


def solution(mesh):
    placed = (P(("pts", "grp"), None, None, None), P(("pts", "grp"), None), P("pts", None))
    return jax.shard_map(
        local,
        mesh=mesh,
        in_specs=placed,
        out_specs=(P("pts", None, "grp"), P("pts", None, "grp")),
        check_vma=False,
    )
```

time: 265 us -> 108 us (0.41); the launches traced: 261 us -> 107 us
  Pallas kernels: 0 us -> 98.2 us
  other arithmetic: 98.6 us -> 1.57 us
  blocking collectives: 61 us -> 0 us
  waiting for transfers between devices: 45.2 us -> 0 us
  matrix products: 19.1 us -> 2.33 us
  between operations: 16.2 us -> 0.65 us
  local copies, waits for them, and re-layouts: 19.3 us -> 4.59 us
    pallas_call x0 -> x1, Pallas kernels: none -> 98.2 us  [local(): pl.pallas_call(functools.partial(kernel, owners, groups, rows_per, width)...]
    another operation x16 -> x0, other arithmetic: 95.3 us -> none  [the longest x10 65.6 us: local(): factor = jnp.linalg.cholesky(system)]
    all_to_all x1 -> x0, blocking collectives: 61 us -> none  [local(): lax.all_to_all(outgoing, 'pts', split_axis=0, concat_axis=0, tiled=True)]
    psum x1 -> x0, waiting for transfers between devices: 40.8 us -> none  [local(): lax.psum((gram(middle, middle), gram(middle, first), gram(middle, last)),...]
    dot_general x9 -> x1, matrix products: 14 us -> 2.33 us  [local(): jnp.einsum('qp,kpf->kqf', pick, planes, preferred_element_type=jnp.float32)]
    another operation x26 -> x0, local copies, waits for them, and re-layouts: 6.45 us -> none  [the longest x16 6 us: local(): lax.linalg.triangular_solve(factor, b_low, left_side=True, lower=True)]
    gather x1 -> x0, local copies, waits for them, and re-layouts: 6.13 us -> none  [local(): jacobian[source]]
    another operation x14 -> x0, matrix products: 5.05 us -> none  [the longest x5 1.92 us: local(): lax.linalg.triangular_solve(factor, b_low, left_side=True, lower=True)]
  transfers between devices with their start and end apart: 5 -> 0, of which waited for: 2 -> 0; matrix products, arithmetic and copies ran while one was open for 44% -> 0% of each run, Pallas kernels for 0% -> 0%
where the time goes in v1:
time: 108 us; the launch traced here: 107 us
  Pallas kernels  98.2 us (91%)
  local copies, waits for them, and re-layouts  4.59 us (4%)
  matrix products  2.33 us (2%)
  other arithmetic  1.57 us (1%)
    pallas_call x1, Pallas kernels, local(): pl.pallas_call(functools.partial(kernel, owners, groups, rows_per, width)...  98.2 us
    unnamed x4, local copies, waits for them, and re-layouts  4.59 us
    dot_general x1, matrix products, local(): jnp.einsum('qp,kpf->kqf', pick, planes, preferred_element_type=jnp.float32)  2.33 us

profile of v1, /device:TPU:0, one launch (start us, length us, event | category | flops | bytes accessed | tf_op | source)
XLA Modules:
  0.0 107.3 jit_solution(5342851632066899282)
XLA Ops:
  0.6 0.0 copy-start
  0.6 1.2 %copy-done = bf16[128,3,3,384]{3,0,2,1:T(8,128)(2,1)S(1)} copy-done((bf16[128,3,3,384]{3,0,2,1:T(8,128)(2,1)S(1)}, bf16[128,3,3,384]{3,0,2,1:T(8,128)(2,1)}, u32[]{:S(2)}) %copy-start) | copy-done | bytes 884760
  1.8 0.8 convert_reduce_fusion
  2.6 0.7 multiply_add_fusion
  3.3 0.1 add_bitcast_fusion
  3.4 2.3 %convert_bitcast_fusion.send = bf16[3,768,384]{2,1,0:T(8,128)(2,1)} fusion(bf16[3,384,384]{2,1,0:T(8,128)(2,1)S(1)} %bitcast.15, s32[384]{0:T(512)S(1)} %add_bitcast_fusion), kind=kOutput, calls=%fused_computation | convolution fusion | flops 680656896 | bytes 2655744 | tf_op jit(solution)/shard_map/qp,kpf->kqf/dot_general | solution.py:302
  5.7 98.2 %shard_map.50 = (f32[384,96]{1,0:T(8,128)}, f32[384,96]{1,0:T(8,128)}) custom-call(bf16[3,768,384]{2,1,0:T(8,128)(2,1)} %convert_bitcast_fusion.send, f32[1,384]{1,0:T(1,128)} %damp.1), custom_call_target="tpu_custom_call" | custom-call | tf_op jit(solution)/shard_map/pallas_call | solution.py:310
  103.9 1.7 %copy.7 = f32[1,384,96]{1,2,0:T(8,128)} copy(f32[1,384,96]{2,1,0:T(8,128)} %bitcast.17) | data formatting | bytes 294912
  105.6 1.7 %copy.8 = f32[1,384,96]{1,2,0:T(8,128)} copy(f32[1,384,96]{2,1,0:T(8,128)} %bitcast.16) | data formatting | bytes 294912
  (1 shorter events, 0.0 us)
Async XLA Ops:
  0.6 1.2 %copy-start = (bf16[128,3,3,384]{3,0,2,1:T(8,128)(2,1)S(1)}, bf16[128,3,3,384]{3,0,2,1:T(8,128)(2,1)}, u32[]{:S(2)}) copy-start(bf16[128,3,3,384]{3,0,2,1:T(8,128)(2,1)} %param.3) | copy-start | bytes 2654212

commit v2 on v1

--- a/solution.py
+++ b/solution.py
@@ -152,18 +152,9 @@
     half = rounds // 2
 
     sides = ((0, 1), (2, 1), (0, 0), (2, 2), (2, 0))
-    count = len(sides)
 
     def chunk_rows(c):
         return pl.ds(pl.multiple_of(c * chunk, TILE), chunk)
-
-    def make_grams():
-        await_rows(0)
-        await_rows(2)
-        for m, (left, right) in enumerate(sides):
-            gram[m] = mm(recv[left], recv[right], TN, False)
-            for h in range(2):
-                near_copy(m, h).start()
 
     def near_copy(m, h):
         return pltpu.make_async_remote_copy(
@@ -172,82 +163,88 @@
             device_id=(me, near), device_id_type=MESH,
         )
 
-    def far_copy(m):
+    def far_copy(m, h):
         return pltpu.make_async_remote_copy(
-            src_ref=gram.at[m, chunk_rows(far)], dst_ref=r2.at[m],
-            send_sem=g_send.at[m, 2], recv_sem=g_recv.at[m, 2],
+            src_ref=gram.at[m, chunk_rows(odd + 2 * h if m < 2 else far)], dst_ref=r2.at[m, h],
+            send_sem=g_send.at[m, 2 + h], recv_sem=g_recv.at[m, 2 + h],
             device_id=(me, far), device_id_type=MESH,
         )
 
-    def fold_near():
-        for m in range(count):
+    def spread_near(m, h):
+        at = chunk_rows(odd + 2 * h)
+        return pltpu.make_async_remote_copy(
+            src_ref=bt.at[m, at], dst_ref=bt.at[m, at],
+            send_sem=b_send.at[m, h], recv_sem=b_recv.at[m, h],
+            device_id=(me, near), device_id_type=MESH,
+        )
+
+    def far_parts(m):
+        return range(2) if m < 2 else range(1)
+
+    def make_grams(k, some):
+        await_rows(k)
+        for m in some:
+            left, right = sides[m]
+            gram[m] = mm(recv[left], recv[right], TN, False)
+            for h in range(2):
+                near_copy(m, h).start()
+
+    def fold_near(some):
+        for m in some:
             for h in range(2):
                 near_copy(m, h).wait()
                 at = chunk_rows(odd + 2 * h)
                 gram[m, at, :] = gram[m, at, :] + r1[m, h]
-            far_copy(m).start()
-
-    def spread_far(m):
-        return pltpu.make_async_remote_copy(
-            src_ref=bt.at[m, chunk_rows(grp)], dst_ref=bt.at[m, chunk_rows(grp)],
-            send_sem=b_send.at[m, 0], recv_sem=b_recv.at[m, 0],
-            device_id=(me, far), device_id_type=MESH,
-        )
-
-    def spread_near(m, h):
-        at = chunk_rows(odd + 2 * h)
-        return pltpu.make_async_remote_copy(
-            src_ref=bt.at[m, at], dst_ref=bt.at[m, at],
-            send_sem=b_send.at[m, 1 + h], recv_sem=b_recv.at[m, 1 + h],
-            device_id=(me, near), device_id_type=MESH,
-        )
-
-    def fold_far():
-        for m in range(count):
-            far_copy(m).wait()
-            at = chunk_rows(grp)
+            for h in far_parts(m):
+                far_copy(m, h).start()
+
+    def fold_far(m):
+        for h in far_parts(m):
+            far_copy(m, h).wait()
             if m < 2:
-                bt[m, at, :] = gram[m, at, :] + r2[m]
-                spread_far(m).start()
+                at = chunk_rows(odd + 2 * h)
+                bt[m, at, :] = gram[m, at, :] + r2[m, h]
+                spread_near(m, h).start()
             else:
-                gram[m, at, :] = gram[m, at, :] + r2[m]
-
-    def spread():
-        for m in range(2):
-            spread_far(m).wait()
-            for h in range(2):
-                spread_near(m, h).start()
-
-    hooks = {(0, 1): make_grams, (1, 0): fold_near, (1, 1): fold_far, (2, 0): spread}
+                at = chunk_rows(grp)
+                gram[m, at, :] = gram[m, at, :] + r2[m, h]
+
+    def second_near():
+        fold_near((1, 3, 4))
+        fold_far(0)
+
+    hooks = {
+        (0, 1): functools.partial(make_grams, 0, (0, 2)),
+        (1, 0): functools.partial(fold_near, (0, 2)),
+        (1, 1): functools.partial(make_grams, 2, (1, 3, 4)),
+        (2, 0): second_near,
+    }
+
+    def block(i, j):
+        if (i, j) not in blocks:
+            blocks[i, j] = reduced(where_in[i, j])
+        return blocks[i, j]
+
     for i in range(nb):
-        for j in range(i, nb):
-            blocks[i, j] = blocks[i, j] if i > 0 else reduced(where_in[i, j])
-        if i == 0:
-            for pair in pairs:
-                if pair[0] > 0:
-                    blocks[pair] = None
-        a = sweep_steps(blocks[i, i], half)
+        a = sweep_steps(block(i, i), half)
         if (i, 0) in hooks:
             hooks.pop((i, 0))()
         a = -sweep_steps(a, rounds - half)
+        inverses.append(a)
+        for j in range(i + 1, nb):
+            factors[i, j] = mm(a, block(i, j), NN, True)
         if (i, 1) in hooks:
             hooks.pop((i, 1))()
-        inverses.append(a)
-        for j in range(i + 1, nb):
-            factors[i, j] = mm(a, blocks[i, j], NN, True)
         for j in range(i + 1, nb):
             for k in range(j, nb):
-                base = blocks[j, k]
-                if base is None:
-                    base = reduced(where_in[j, k])
-                blocks[j, k] = base - mm(blocks[i, j], factors[i, k], TN, True)
+                blocks[j, k] = block(j, k) - mm(block(i, j), factors[i, k], TN, True)
     for key in sorted(hooks):
         hooks[key]()
-    for m in range(2):
+    mine = chunk_rows(grp)
+
+    def eliminate(m):
         for h in range(2):
             spread_near(m, h).wait()
-
-    for m in range(2):
         for j in range(1, nb):
             value = bt[m, :, j * LANES : (j + 1) * LANES]
             for i in range(j):
@@ -255,33 +252,35 @@
                     bt[m, :, i * LANES : (i + 1) * LANES], factors[i, j], NN, True
                 )
             bt[m, :, j * LANES : (j + 1) * LANES] = value
-    mine = chunk_rows(grp)
-    solved = []
-    for m in range(2):
-        solved.append(
-            jnp.concatenate(
-                [
-                    mm(bt[m, mine, i * LANES : (i + 1) * LANES], inverses[i], NN, True)
-                    for i in range(nb)
-                ],
-                1,
-            )
-        )
-    highs[...] = gram[3, mine, :] - mm(solved[1], bt[1], NT, True)
+        return jnp.concatenate(
+            [
+                mm(bt[m, mine, i * LANES : (i + 1) * LANES], inverses[i], NN, True)
+                for i in range(nb)
+            ],
+            1,
+        )
+
+    solved_low = eliminate(0)
+    fold_far(1)
+    fold_far(2)
+    diag_out[...] = gram[2, mine, :] - mm(solved_low, bt[0], NT, True)
+    solved_high = eliminate(1)
+    fold_far(3)
+    highs[...] = gram[3, mine, :] - mm(solved_high, bt[1], NT, True)
     carry = pltpu.make_async_remote_copy(
         src_ref=highs, dst_ref=carried, send_sem=c_send, recv_sem=c_recv,
         device_id=(lax.rem(me + 1, owners), grp), device_id_type=MESH,
     )
     carry.start()
-    low = gram[2, mine, :] - mm(solved[0], bt[0], NT, True)
-    pair_out[...] = (gram[4, mine, :] - mm(solved[1], bt[0], NT, True)).T
+    fold_far(4)
+    pair_out[...] = gram[4, mine, :] - mm(solved_high, bt[0], NT, True)
     for copy in first_copies + second_copies:
         copy.wait_send()
     for k in range(3):
         part = send.at[k, pl.ds(0, (owners - 1) * rows_per)]
         pltpu.make_async_copy(part, part, a_send.at[k]).wait()
     carry.wait()
-    diag_out[...] = (low + carried[...]).T
+    diag_out[...] = diag_out[...] + carried[...]
 
 
 def local(jacobian, owner, damping):
@@ -309,7 +308,7 @@
     dma = pltpu.SemaphoreType.DMA
     diag, pair = pl.pallas_call(
         functools.partial(kernel, owners, groups, rows_per, width),
-        out_shape=[jax.ShapeDtypeStruct((width, chunk), jnp.float32)] * 2,
+        out_shape=[jax.ShapeDtypeStruct((chunk, width), jnp.float32)] * 2,
         in_specs=[vmem, vmem],
         out_specs=[vmem, vmem],
         scratch_shapes=[
@@ -319,19 +318,19 @@
             pltpu.VMEM((blocks, LANES, LANES), jnp.float32),
             pltpu.VMEM((5, width, width), jnp.float32),
             pltpu.VMEM((5, 2, chunk, width), jnp.float32),
-            pltpu.VMEM((5, chunk, width), jnp.float32),
+            pltpu.VMEM((5, 2, chunk, width), jnp.float32),
             pltpu.VMEM((2, width, width), jnp.float32),
             pltpu.VMEM((chunk, width), jnp.float32),
             pltpu.VMEM((chunk, width), jnp.float32),
             dma((3,)), dma((3,)),
             dma((2 * blocks,)), dma((blocks,)), dma((blocks,)),
-            dma((5, 3)), dma((5, 3)),
-            dma((2, 3)), dma((2, 3)),
+            dma((5, 4)), dma((5, 4)),
+            dma((2, 2)), dma((2, 2)),
             dma, dma, dma((3,)),
         ],
         compiler_params=pltpu.CompilerParams(collective_id=0, has_side_effects=True),
     )(outgoing, damping)
-    return diag[None], pair[None]
+    return diag.T[None], pair.T[None]
 
 
 def solution(mesh):

time: 108 us -> 97.2 us (0.900)
  Pallas kernels: 98.2 us -> 88.1 us
    pallas_call x1, Pallas kernels: 98.2 us -> 88.1 us  [local(): pl.pallas_call(functools.partial(kernel, owners, groups, rows_per, width)...]
where the time goes in v2:
time: 97.2 us; the launch traced here: 96.9 us
  Pallas kernels  88.1 us (91%)
  local copies, waits for them, and re-layouts  4.33 us (4%)
  matrix products  2.33 us (2%)
  other arithmetic  1.57 us (2%)
    pallas_call x1, Pallas kernels, local(): pl.pallas_call(functools.partial(kernel, owners, groups, rows_per, width)...  88.1 us
    unnamed x4, local copies, waits for them, and re-layouts  4.33 us
    dot_general x1, matrix products, local(): jnp.einsum('qp,kpf->kqf', pick, planes, preferred_element_type=jnp.float32)  2.33 us

profile of v2, /device:TPU:0, one launch (start us, length us, event | category | flops | bytes accessed | tf_op | source)
XLA Modules:
  0.0 96.9 jit_solution(8185482393378128800)
XLA Ops:
  0.6 0.0 copy-start
  0.6 1.2 %copy-done = bf16[128,3,3,384]{3,0,2,1:T(8,128)(2,1)S(1)} copy-done((bf16[128,3,3,384]{3,0,2,1:T(8,128)(2,1)S(1)}, bf16[128,3,3,384]{3,0,2,1:T(8,128)(2,1)}, u32[]{:S(2)}) %copy-start) | copy-done | bytes 884760
  1.8 0.8 convert_reduce_fusion
  2.6 0.7 multiply_add_fusion
  3.3 0.1 add_bitcast_fusion
  3.4 2.3 %convert_bitcast_fusion.send = bf16[3,768,384]{2,1,0:T(8,128)(2,1)} fusion(bf16[3,384,384]{2,1,0:T(8,128)(2,1)S(1)} %bitcast.19, s32[384]{0:T(512)S(1)} %add_bitcast_fusion), kind=kOutput, calls=%fused_computation | convolution fusion | flops 680656896 | bytes 2655744 | tf_op jit(solution)/shard_map/qp,kpf->kqf/dot_general | solution.py:301
  5.7 88.1 %shard_map.50 = (f32[96,384]{1,0:T(8,128)}, f32[96,384]{1,0:T(8,128)}) custom-call(bf16[3,768,384]{2,1,0:T(8,128)(2,1)} %convert_bitcast_fusion.send, f32[1,384]{1,0:T(1,128)} %damp.1), custom_call_target="tpu_custom_call" | custom-call | tf_op jit(solution)/shard_map/pallas_call | solution.py:309
  93.8 1.6 %copy.7 = f32[1,384,96]{1,2,0:T(8,128)} copy(f32[1,384,96]{1,2,0:T(8,128)} %bitcast.21) | data formatting | bytes 294912
  95.4 1.6 %copy.8 = f32[1,384,96]{1,2,0:T(8,128)} copy(f32[1,384,96]{1,2,0:T(8,128)} %bitcast.20) | data formatting | bytes 294912
  (1 shorter events, 0.0 us)
Async XLA Ops:
  0.6 1.2 %copy-start = (bf16[128,3,3,384]{3,0,2,1:T(8,128)(2,1)S(1)}, bf16[128,3,3,384]{3,0,2,1:T(8,128)(2,1)}, u32[]{:S(2)}) copy-start(bf16[128,3,3,384]{3,0,2,1:T(8,128)(2,1)} %param.3) | copy-start | bytes 2654212

commit v3 on v2

--- a/solution.py
+++ b/solution.py
@@ -48,9 +48,9 @@
 
 
 def kernel(
-    owners, groups, rows_per, width,
-    send, damp, diag_out, pair_out,
-    recv, sblk, s1, s2, gram, r1, r2, bt, highs, carried,
+    owners, groups, rows_per, width, capacity,
+    planes, owner_row, damp, low_out, pair_out, carried,
+    send, recv, sblk, s1, s2, gram, r1, r2, bt, highs,
     a_send, a_recv, d_send, d_recv, d2_recv, g_send, g_recv, b_send, b_recv, c_send, c_recv, own_sem,
 ):
     me = lax.axis_index("pts")
@@ -73,12 +73,33 @@
     lax.fori_loop(1, owners, greet, 0)
     for other in (near, far):
         pl.semaphore_signal(barrier, inc=1, device_id=(me, other), device_id_type=MESH)
+
+    clusters, spots, _ = planes.shape
+    points = owner_row.shape[1]
+    earlier = (
+        lax.broadcasted_iota(jnp.int32, (points, points), 0)
+        < lax.broadcasted_iota(jnp.int32, (points, points), 1)
+    )
+    spread = jnp.broadcast_to(owner_row[...], (points, points))
+    ahead = jnp.where((spread.T == spread) & earlier, 1, 0)
+    place = owner_row[...] * rows_per + jnp.sum(ahead, axis=0, keepdims=True)
+    place = jnp.concatenate([place + capacity * r for r in range(spots // points)], 1)
+    slot = lax.broadcasted_iota(jnp.int32, (owners * rows_per, spots), 0)
+    pick = jnp.where(slot == place, 1.0, 0.0).astype(send.dtype)
+
+    def pack(k):
+        send[k] = mm(pick, planes[k], NN, False).astype(send.dtype)
+
+    pack(1)
     pl.semaphore_wait(barrier, owners - 1 + 2)
 
     def rows_at(i):
         return pl.ds(pl.multiple_of(i * rows_per, rows_per), rows_per)
 
     for k in (1, 0, 2):
+        if k != 1:
+            pack(k)
+
         def issue(off, _, k=k):
             to = lax.rem(me + off, owners)
             pltpu.make_async_remote_copy(
@@ -107,30 +128,36 @@
 
     await_rows(1)
     first_copies = []
-    for n, (i, j) in enumerate(pairs):
-        sblk[n] = mm(
-            recv[1, :, i * LANES : (i + 1) * LANES],
-            recv[1, :, j * LANES : (j + 1) * LANES], TN, False,
-        )
-        copy = pltpu.make_async_remote_copy(
-            src_ref=sblk.at[n], dst_ref=s1.at[n],
-            send_sem=d_send.at[n], recv_sem=d_recv.at[n],
-            device_id=(me, near), device_id_type=MESH,
-        )
-        copy.start()
-        first_copies.append(copy)
+    own = len(pairs)
+    for i in range(nb):
+        strip = mm(
+            recv[1, :, i * LANES : (i + 1) * LANES], recv[1, :, i * LANES :], TN, False
+        )
+        for j in range(i, nb):
+            n = pairs.index((i, j))
+            sblk[n] = strip[:, (j - i) * LANES : (j - i + 1) * LANES]
+            copy = pltpu.make_async_remote_copy(
+                src_ref=sblk.at[n], dst_ref=s1.at[n],
+                send_sem=d_send.at[n], recv_sem=d_recv.at[n],
+                device_id=(me, near), device_id_type=MESH,
+            )
+            copy.start()
+            first_copies.append(copy)
     second_copies = []
-    own = len(pairs)
-    for n in range(own):
-        first_copies[n].wait_recv()
-        sblk[own + n] = sblk[n] + s1[n]
-        copy = pltpu.make_async_remote_copy(
-            src_ref=sblk.at[own + n], dst_ref=s2.at[n],
-            send_sem=d_send.at[own + n], recv_sem=d2_recv.at[n],
-            device_id=(me, far), device_id_type=MESH,
-        )
-        copy.start()
-        second_copies.append(copy)
+
+    def forward(some):
+        for n in some:
+            first_copies[n].wait_recv()
+            sblk[own + n] = sblk[n] + s1[n]
+            copy = pltpu.make_async_remote_copy(
+                src_ref=sblk.at[own + n], dst_ref=s2.at[n],
+                send_sem=d_send.at[own + n], recv_sem=d2_recv.at[n],
+                device_id=(me, far), device_id_type=MESH,
+            )
+            copy.start()
+            second_copies.append(copy)
+
+    forward(range(1))
 
     eye = (
         lax.broadcasted_iota(jnp.int32, (LANES, LANES), 0)
@@ -214,6 +241,7 @@
         fold_far(0)
 
     hooks = {
+        (0, 0): functools.partial(forward, range(1, own)),
         (0, 1): functools.partial(make_grams, 0, (0, 2)),
         (1, 0): functools.partial(fold_near, (0, 2)),
         (1, 1): functools.partial(make_grams, 2, (1, 3, 4)),
@@ -226,10 +254,11 @@
         return blocks[i, j]
 
     for i in range(nb):
-        a = sweep_steps(block(i, i), half)
+        head = half if i > 0 else half // 2
+        a = sweep_steps(block(i, i), head)
         if (i, 0) in hooks:
             hooks.pop((i, 0))()
-        a = -sweep_steps(a, rounds - half)
+        a = -sweep_steps(a, rounds - head)
         inverses.append(a)
         for j in range(i + 1, nb):
             factors[i, j] = mm(a, block(i, j), NN, True)
@@ -263,7 +292,7 @@
     solved_low = eliminate(0)
     fold_far(1)
     fold_far(2)
-    diag_out[...] = gram[2, mine, :] - mm(solved_low, bt[0], NT, True)
+    low_out[...] = gram[2, mine, :] - mm(solved_low, bt[0], NT, True)
     solved_high = eliminate(1)
     fold_far(3)
     highs[...] = gram[3, mine, :] - mm(solved_high, bt[1], NT, True)
@@ -280,7 +309,11 @@
         part = send.at[k, pl.ds(0, (owners - 1) * rows_per)]
         pltpu.make_async_copy(part, part, a_send.at[k]).wait()
     carry.wait()
-    diag_out[...] = diag_out[...] + carried[...]
+
+
+def finish(low, pair, carried, diag_out, pair_out):
+    diag_out[...] = low[...] + carried[...]
+    pair_out[...] = pair[...]
 
 
 def local(jacobian, owner, damping):
@@ -290,28 +323,19 @@
     capacity = max(2, 2 * points // owners)
     rows_per = -(-residuals * capacity // 16) * 16
     total = owners * rows_per
-    segment = owner[:, 0]
-    same = segment[:, None] == segment[None, :]
-    before = jnp.arange(points)[:, None] < jnp.arange(points)[None, :]
-    rank = jnp.sum((same & before).astype(jnp.int32), axis=0)
-    place = segment * rows_per + rank
-    place = (place[None, :] + capacity * jnp.arange(residuals)[:, None]).reshape(-1)
-    pick = (jnp.arange(total)[:, None] == place[None, :]).astype(jacobian.dtype)
     planes = jnp.transpose(jacobian, (1, 2, 0, 3)).reshape(clusters, residuals * points, width)
-    outgoing = jnp.einsum(
-        "qp,kpf->kqf", pick, planes, preferred_element_type=jnp.float32
-    ).astype(jacobian.dtype)
     chunk = width // groups
     nb = width // LANES
     blocks = nb * (nb + 1) // 2
     vmem = pl.BlockSpec(memory_space=pltpu.VMEM)
     dma = pltpu.SemaphoreType.DMA
-    diag, pair = pl.pallas_call(
-        functools.partial(kernel, owners, groups, rows_per, width),
-        out_shape=[jax.ShapeDtypeStruct((chunk, width), jnp.float32)] * 2,
-        in_specs=[vmem, vmem],
-        out_specs=[vmem, vmem],
+    low, pair, carried = pl.pallas_call(
+        functools.partial(kernel, owners, groups, rows_per, width, capacity),
+        out_shape=[jax.ShapeDtypeStruct((chunk, width), jnp.float32)] * 3,
+        in_specs=[vmem] * 3,
+        out_specs=[vmem] * 3,
         scratch_shapes=[
+            pltpu.VMEM((clusters, total, width), jacobian.dtype),
             pltpu.VMEM((clusters, total, width), jacobian.dtype),
             pltpu.VMEM((2 * blocks, LANES, LANES), jnp.float32),
             pltpu.VMEM((blocks, LANES, LANES), jnp.float32),
@@ -321,7 +345,6 @@
             pltpu.VMEM((5, 2, chunk, width), jnp.float32),
             pltpu.VMEM((2, width, width), jnp.float32),
             pltpu.VMEM((chunk, width), jnp.float32),
-            pltpu.VMEM((chunk, width), jnp.float32),
             dma((3,)), dma((3,)),
             dma((2 * blocks,)), dma((blocks,)), dma((blocks,)),
             dma((5, 4)), dma((5, 4)),
@@ -329,7 +352,13 @@
             dma, dma, dma((3,)),
         ],
         compiler_params=pltpu.CompilerParams(collective_id=0, has_side_effects=True),
-    )(outgoing, damping)
+    )(planes, owner.reshape(1, points), damping)
+    diag, pair = pl.pallas_call(
+        finish,
+        out_shape=[jax.ShapeDtypeStruct((chunk, width), jnp.float32)] * 2,
+        in_specs=[vmem] * 3,
+        out_specs=[vmem] * 2,
+    )(low, pair, carried)
     return diag.T[None], pair.T[None]
 
 

time: 97.2 us -> 89.8 us (0.924)
  local copies, waits for them, and re-layouts: 4.33 us -> 0 us
  matrix products: 2.33 us -> 0 us
  other arithmetic: 1.57 us -> 0 us
    unnamed x4 -> x0, local copies, waits for them, and re-layouts: 4.33 us -> none
    dot_general x1 -> x0, matrix products: 2.33 us -> none  [local(): jnp.einsum('qp,kpf->kqf', pick, planes, preferred_element_type=jnp.float32)]
    pallas_call x1 -> x2, Pallas kernels: 88.1 us -> 89 us  [the longest x1 87.2 us: local(): pl.pallas_call(functools.partial(kernel, owners, groups, rows_per, width,...]
where the time goes in v3:
time: 89.8 us; the launch traced here: 89.6 us
  Pallas kernels  89 us (99%)
    pallas_call x1, Pallas kernels, local(): pl.pallas_call(functools.partial(kernel, owners, groups, rows_per, width,...  87.2 us

profile of v3, /device:TPU:0, one launch (start us, length us, event | category | flops | bytes accessed | tf_op | source)
XLA Modules:
  0.0 89.6 jit_solution(18246517112204620048)
XLA Ops:
  0.6 87.2 %shard_map.50 = (f32[96,384]{1,0:T(8,128)}, f32[96,384]{1,0:T(8,128)}, f32[96,384]{1,0:T(8,128)}) custom-call(bf16[3,384,384]{2,1,0:T(8,128)(2,1)} %bitcast.10, s32[1,128]{1,0:T(1,128)} %bitcast.11, f32[1,384]{1,0:T(1,128)} %damp.1), custom_call_target="tpu_custom_call" | custom-call | tf_op jit(solution)/shard_map/pallas_call | solution.py:332
  87.8 1.8 %shard_map.51 = (f32[96,384]{1,0:T(8,128)}, f32[96,384]{1,0:T(8,128)}) custom-call(f32[96,384]{1,0:T(8,128)} %get-tuple-element.7.low, f32[96,384]{1,0:T(8,128)} %get-tuple-element.8.pair, f32[96,384]{1,0:T(8,128)} %get-tuple-element.9.carried), custom_call_target="tpu_custom_call" | custom-call | tf_op jit(solution)/shard_map/pallas_call | solution.py:356

commit v4 on v3

--- a/solution.py
+++ b/solution.py
@@ -37,9 +37,10 @@
         for t in range(TILE):
             row = a[t : t + 1, :]
             col = a[:, t : t + 1]
-            scaled = jnp.where(lane_row == t, -1.0, row) * (1.0 / a[t : t + 1, t : t + 1])
-            new = jnp.where(lane == t, 0.0, a) - col * scaled
-            top = jnp.where(top_row == t, scaled, new[:TILE])
+            inverse = 1.0 / a[t : t + 1, t : t + 1]
+            marked = jnp.where(lane_row == t, -1.0, row)
+            new = jnp.where(lane == t, 0.0, a) - (col * marked) * inverse
+            top = jnp.where(top_row == t, marked * inverse, new[:TILE])
             a = jnp.concatenate([top, new[TILE:]], 0)
         a = pltpu.roll(a, size - TILE, 1)
         return jnp.concatenate([a[TILE:], a[:TILE]], 0)
@@ -176,7 +177,6 @@
     blocks = {}
     inverses, factors = [], {}
     rounds = LANES // TILE
-    half = rounds // 2
 
     sides = ((0, 1), (2, 1), (0, 0), (2, 2), (2, 0))
 
@@ -237,15 +237,19 @@
                 gram[m, at, :] = gram[m, at, :] + r2[m, h]
 
     def second_near():
-        fold_near((1, 3, 4))
+        fold_near((1,))
         fold_far(0)
 
+    quarters = 4
     hooks = {
-        (0, 0): functools.partial(forward, range(1, own)),
-        (0, 1): functools.partial(make_grams, 0, (0, 2)),
-        (1, 0): functools.partial(fold_near, (0, 2)),
-        (1, 1): functools.partial(make_grams, 2, (1, 3, 4)),
-        (2, 0): second_near,
+        (0, 1): functools.partial(forward, range(1, own)),
+        (0, quarters): functools.partial(make_grams, 0, (0, 2)),
+        (1, 1): functools.partial(fold_near, (0,)),
+        (1, 2): functools.partial(fold_near, (2,)),
+        (1, quarters): functools.partial(make_grams, 2, (1, 3, 4)),
+        (2, 1): second_near,
+        (2, 2): functools.partial(fold_near, (3,)),
+        (2, 3): functools.partial(fold_near, (4,)),
     }
 
     def block(i, j):
@@ -254,16 +258,17 @@
         return blocks[i, j]
 
     for i in range(nb):
-        head = half if i > 0 else half // 2
-        a = sweep_steps(block(i, i), head)
-        if (i, 0) in hooks:
-            hooks.pop((i, 0))()
-        a = -sweep_steps(a, rounds - head)
+        a = block(i, i)
+        for part in range(1, quarters + 1):
+            a = sweep_steps(a, rounds // quarters)
+            if part < quarters and (i, part) in hooks:
+                hooks.pop((i, part))()
+        a = -a
         inverses.append(a)
         for j in range(i + 1, nb):
             factors[i, j] = mm(a, block(i, j), NN, True)
-        if (i, 1) in hooks:
-            hooks.pop((i, 1))()
+        if (i, quarters) in hooks:
+            hooks.pop((i, quarters))()
         for j in range(i + 1, nb):
             for k in range(j, nb):
                 blocks[j, k] = block(j, k) - mm(block(i, j), factors[i, k], TN, True)
@@ -289,8 +294,8 @@
             1,
         )
 
+    fold_far(1)
     solved_low = eliminate(0)
-    fold_far(1)
     fold_far(2)
     low_out[...] = gram[2, mine, :] - mm(solved_low, bt[0], NT, True)
     solved_high = eliminate(1)

time: 89.8 us -> 100 us (1.11)
  Pallas kernels: 89 us -> 99.4 us
    pallas_call x1, Pallas kernels: 87.2 us -> 97.6 us  [local(): pl.pallas_call(functools.partial(kernel, owners, groups, rows_per, width,...]
where the time goes in v4:
time: 100 us
  Pallas kernels  99.4 us (99%)
    pallas_call x1, Pallas kernels, local(): pl.pallas_call(functools.partial(kernel, owners, groups, rows_per, width,...  97.6 us

profile of v4, /device:TPU:0, one launch (start us, length us, event | category | flops | bytes accessed | tf_op | source)
XLA Modules:
  0.0 100.0 jit_solution(5365742823840201669)
XLA Ops:
  0.6 97.6 %shard_map.50 = (f32[96,384]{1,0:T(8,128)}, f32[96,384]{1,0:T(8,128)}, f32[96,384]{1,0:T(8,128)}) custom-call(bf16[3,384,384]{2,1,0:T(8,128)(2,1)} %bitcast.10, s32[1,128]{1,0:T(1,128)} %bitcast.11, f32[1,384]{1,0:T(1,128)} %damp.1), custom_call_target="tpu_custom_call" | custom-call | tf_op jit(solution)/shard_map/pallas_call | solution.py:337
  98.2 1.8 %shard_map.51 = (f32[96,384]{1,0:T(8,128)}, f32[96,384]{1,0:T(8,128)}) custom-call(f32[96,384]{1,0:T(8,128)} %get-tuple-element.7.low, f32[96,384]{1,0:T(8,128)} %get-tuple-element.8.pair, f32[96,384]{1,0:T(8,128)} %get-tuple-element.9.carried), custom_call_target="tpu_custom_call" | custom-call | tf_op jit(solution)/shard_map/pallas_call | solution.py:361

commit v5 on v4

--- a/solution.py
+++ b/solution.py
@@ -37,10 +37,9 @@
         for t in range(TILE):
             row = a[t : t + 1, :]
             col = a[:, t : t + 1]
-            inverse = 1.0 / a[t : t + 1, t : t + 1]
-            marked = jnp.where(lane_row == t, -1.0, row)
-            new = jnp.where(lane == t, 0.0, a) - (col * marked) * inverse
-            top = jnp.where(top_row == t, marked * inverse, new[:TILE])
+            scaled = jnp.where(lane_row == t, -1.0, row) * (1.0 / a[t : t + 1, t : t + 1])
+            new = jnp.where(lane == t, 0.0, a) - col * scaled
+            top = jnp.where(top_row == t, scaled, new[:TILE])
             a = jnp.concatenate([top, new[TILE:]], 0)
         a = pltpu.roll(a, size - TILE, 1)
         return jnp.concatenate([a[TILE:], a[:TILE]], 0)

time: 100 us -> 88.1 us (0.88)
  Pallas kernels: 99.4 us -> 87.3 us
    pallas_call x1, Pallas kernels: 97.6 us -> 85.5 us  [local(): pl.pallas_call(functools.partial(kernel, owners, groups, rows_per, width,...]
where the time goes in v5:
time: 88.1 us; the launch traced here: 87.9 us
  Pallas kernels  87.3 us (99%)
    pallas_call x1, Pallas kernels, local(): pl.pallas_call(functools.partial(kernel, owners, groups, rows_per, width,...  85.5 us
    pallas_call x1, Pallas kernels, local(): pl.pallas_call(finish, out_shape=[jax.ShapeDtypeStruct((chunk, width), jn...  1.78 us

profile of v5, /device:TPU:0, one launch (start us, length us, event | category | flops | bytes accessed | tf_op | source)
XLA Modules:
  0.0 87.9 jit_solution(2698070060131287933)
XLA Ops:
  0.6 85.5 %shard_map.50 = (f32[96,384]{1,0:T(8,128)}, f32[96,384]{1,0:T(8,128)}, f32[96,384]{1,0:T(8,128)}) custom-call(bf16[3,384,384]{2,1,0:T(8,128)(2,1)} %bitcast.10, s32[1,128]{1,0:T(1,128)} %bitcast.11, f32[1,384]{1,0:T(1,128)} %damp.1), custom_call_target="tpu_custom_call" | custom-call | tf_op jit(solution)/shard_map/pallas_call | solution.py:336
  86.2 1.8 %shard_map.51 = (f32[96,384]{1,0:T(8,128)}, f32[96,384]{1,0:T(8,128)}) custom-call(f32[96,384]{1,0:T(8,128)} %get-tuple-element.7.low, f32[96,384]{1,0:T(8,128)} %get-tuple-element.8.pair, f32[96,384]{1,0:T(8,128)} %get-tuple-element.9.carried), custom_call_target="tpu_custom_call" | custom-call | tf_op jit(solution)/shard_map/pallas_call | solution.py:360
